TPU v7x, 32 devices: a whole 2x2x4 slice. The times are simulated.
32 devices in a mesh: seq: 2 (over x), mp: 4 (over y, core), dp: 4 (over z).
Axes of the slice: x: 2, y: 2, z: 4, core: 2. Of those that a mesh axis runs over, the one named last changes fastest.
Arguments:
- tokens: bfloat16 [16384, 2048], P(('dp', 'seq'), 'mp'), parts along dimension 0, may hold values from -6 to 6
- w_query: bfloat16 [2048, 2048], P(None, 'mp'), may hold values from -0.125 to 0.125
- w_key: bfloat16 [2048, 2048], P(None, 'mp'), may hold values from -0.125 to 0.125
- w_value: bfloat16 [2048, 2048], P(None, 'mp'), may hold values from -0.125 to 0.125
- w_gate: bfloat16 [2048, 2048], P(None, 'mp'), may hold values from -0.125 to 0.125
- decay_exponent: int32 [16], P('mp'), may hold values from 5 to 16
- forget: float32 [16384, 16], P(('dp', 'seq'), 'mp'), parts along dimension 0, may hold values from 0 to 0.69
- norm_gain: float32 [2048], replicated, may hold values from 0.1 to 1.9
Outputs:
- retained: bfloat16 [16384, 2048], P(('dp', 'seq', 'mp')), parts along dimension 0
There are 4 independent parts, one for each index of `dp`. A program takes and returns all parts, laid end to end along the dimension named above; an argument that names none is the same for every part. Nothing has to cross between parts.
All inputs are finite; a program needn't handle non-finite values.
Results may differ from a plain program's by a relative error of at most 0.015.
Values may be sent and summed in bfloat16 or wider, within the bound.
No kernel may reach another device: no remote copies, remote signals or barrier semaphores. Data moves between devices by JAX's collectives and lax.ppermute only.
A program may use at most 64 MiB of HBM per device.

v0:
```python
import jax
import jax.numpy as jnp
from jax import lax
from jax.sharding import PartitionSpec as P

DH = 128


def carried_in(shard, axis, join, neutral):
    place = lax.axis_index(axis)
    gathered = jax.tree.map(
        lambda a, kind: lax.all_gather(a.astype(kind), axis), shard, (jnp.bfloat16, jnp.bfloat16)
    )
    state = jax.tree.map(lambda a, e: jnp.zeros_like(a) + jnp.asarray(e, a.dtype), shard, neutral)

    def one(hop, state):
        return join(
            state,
            jax.tree.map(
                lambda a, own: lax.dynamic_index_in_dim(a, hop, 0, False).astype(own.dtype),
                gathered,
                shard,
            ),
        )

    return lax.fori_loop(0, place, one, state)


def run_blocks(queries, key_rows, values, logdecay, head_count, head_width):
    seq_rows = queries.shape[0]
    block_rows = 512
    block_count = seq_rows // block_rows

    def shaped(source):
        return source.reshape(block_count, block_rows, head_count, head_width)

    decays = logdecay.reshape(block_count, block_rows, head_count)
    position = lax.broadcasted_iota(jnp.int32, (block_rows, block_rows), 0)
    earlier = lax.broadcasted_iota(jnp.int32, (block_rows, block_rows), 1)
    causal = position >= earlier

    def advance(carried, pieces):
        kv_state, offset = carried
        query_blk, key_blk, value_blk, decay_blk = pieces
        running = jnp.cumsum(decay_blk, axis=0)
        heads_first = running.T
        log_gap = heads_first[:, :, None] - heads_first[:, None, :]
        decay_mask = jnp.where(causal[None], jnp.exp(jnp.where(causal[None], log_gap, 0.0)), 0.0)
        scores = jnp.einsum("tha,sha->hts", query_blk, key_blk, preferred_element_type=jnp.float32)
        scores = (scores * decay_mask).astype(jnp.bfloat16)
        inner = jnp.einsum("hts,shb->thb", scores, value_blk, preferred_element_type=jnp.float32)
        query_float = query_blk.astype(jnp.float32)
        earlier_part = jnp.einsum(
            "tha,hab->thb",
            query_float * jnp.exp(running)[:, :, None],
            kv_state,
            precision=lax.Precision.HIGHEST,
        )
        query_device = query_float * jnp.exp(running + offset[None, :])[:, :, None]
        key_scaled = key_blk.astype(jnp.float32) * jnp.exp(running[-1:] - running)[:, :, None]
        kv_state = jnp.exp(running[-1])[:, None, None] * kv_state + jnp.einsum(
            "sha,shb->hab",
            key_scaled,
            value_blk.astype(jnp.float32),
            precision=lax.Precision.HIGHEST,
        )
        return ((kv_state, offset + running[-1]), (inner + earlier_part, query_device))

    initial = (
        jnp.zeros((head_count, head_width, head_width), jnp.float32),
        jnp.zeros((head_count,), jnp.float32),
    )
    final, outputs = lax.scan(
        advance, initial, (shaped(queries), shaped(key_rows), shaped(values), decays)
    )
    local_part = outputs[0].reshape(seq_rows, head_count, head_width)
    query_device = outputs[1].reshape(seq_rows, head_count, head_width)
    return (local_part, query_device, final[0], final[1])


def combine_states(before, after):
    return (before[0] * after[0], after[0][:, None, None] * before[1] + after[1])


def body(tokens, w_query, w_key, w_value, w_gate, decay_exponent, forget, norm_gain):
    seq_rows = tokens.shape[0]
    local_width = w_query.shape[1]
    head_count = decay_exponent.shape[0]
    head_width = local_width // head_count
    empty = jnp.zeros((seq_rows, local_width), jnp.float32)
    summed = (empty, empty, empty, empty)
    piece = lax.all_gather(tokens, "mp", axis=1, tiled=True)
    results = []
    for weight, partial_value in zip((w_query, w_key, w_value, w_gate), summed):
        results.append(jnp.dot(piece, weight, preferred_element_type=jnp.float32))
    projected = tuple(results)
    queries = projected[0].astype(jnp.bfloat16)
    key_rows = (projected[1] * DH ** (-0.5)).astype(jnp.bfloat16)
    values = projected[2].astype(jnp.bfloat16)
    gate = projected[3].astype(jnp.bfloat16)
    rate = jnp.log1p(-jnp.exp2(-decay_exponent.astype(jnp.float32)))
    logdecay = rate[None, :] - forget
    local_part, query_device, own_state, own_total = run_blocks(
        queries, key_rows, values, logdecay, head_count, head_width
    )
    prefix = carried_in(
        (jnp.exp(own_total), own_state),
        "seq",
        combine_states,
        (jnp.ones_like(own_total), jnp.zeros_like(own_state)),
    )
    incoming = prefix[1]
    from_before = jnp.einsum(
        "tha,hab->thb", query_device, incoming, precision=lax.Precision.HIGHEST
    )
    output = (local_part + from_before).astype(jnp.bfloat16).reshape(seq_rows, local_width)
    moved_output, moved_gate = (
        lax.all_to_all(output, "mp", split_axis=0, concat_axis=1, tiled=True),
        lax.all_to_all(gate, "mp", split_axis=0, concat_axis=1, tiled=True),
    )
    output_float = moved_output.astype(jnp.float32)
    rstd = lax.rsqrt(jnp.mean(output_float * output_float, axis=1) + 1e-06)
    gated = (
        jax.nn.silu(moved_gate.astype(jnp.float32))
        * output_float
        * rstd[:, None]
        * norm_gain[None, :]
    )
    return gated.astype(jnp.bfloat16)


def solution(mesh):
    placed = (
        P(("dp", "seq"), "mp"),
        P(None, "mp"),
        P(None, "mp"),
        P(None, "mp"),
        P(None, "mp"),
        P("mp"),
        P(("dp", "seq"), "mp"),
        P(),
    )
    return jax.shard_map(
        body, mesh=mesh, in_specs=placed, out_specs=P(("dp", "seq", "mp"), None), check_vma=False
    )
```

profile of v0, /device:TPU:0, one launch (start us, length us, event | category | flops | bytes accessed | tf_op | source)
XLA Modules:
  0.0 337.5 jit_solution(5486481289894038509)
XLA Ops:
  6.5 0.7 all-gather.4.cloned.1.call-update
  7.3 1.2 dynamic-slice
  9.2 0.7 negate_log-plus-one_fusion
  9.9 0.8 broadcast_subtract_fusion
  10.7 59.2 %all-gather.4.cloned.1.call-done = bf16[2048,2048]{1,0:T(8,128)(2,1)} async-done(((bf16[2048,512]{1,0:T(8,128)(2,1)}), bf16[2048,2048]{1,0:T(8,128)(2,1)}) %all-gather.4.cloned.1.call-update) | async-done | bytes 8388624 | tf_op jit(solution)/shard_map/all_gather | solution.py:92
  69.9 9.1 %convolution_convert_fusion = bf16[2048,512]{1,0:T(8,128)(2,1)} fusion(bf16[2048,2048]{1,0:T(8,128)(2,1)} %all-gather.4.cloned.1.call-done, bf16[2048,512]{1,0:T(8,128)(2,1)S(1)} %copy-done), kind=kOutput, calls=%fused_computation.48 | convolution fusion | flops 4296015872 | bytes 12582912 | tf_op jit(solution)/shard_map/dot_general | solution.py:95
  79.0 4.0 %reshape.90 = bf16[4,512,4,128]{3,2,1,0:T(4,128)(2,1)} reshape(bf16[2048,512]{1,0:T(8,128)(2,1)} %convolution_convert_fusion) | data formatting | bytes 4194304 | tf_op jit(solution)/shard_map/reshape | solution.py:35
  83.0 8.5 %convolution_convert_fusion.1 = bf16[2048,512]{1,0:T(8,128)(2,1)S(1)} fusion(bf16[2048,2048]{1,0:T(8,128)(2,1)} %all-gather.4.cloned.1.call-done, bf16[2048,512]{1,0:T(8,128)(2,1)} %param.15), kind=kOutput, calls=%fused_computation.49 | convolution fusion | flops 4296015872 | bytes 12582912 | tf_op jit(solution)/shard_map/dot_general | solution.py:95
  91.5 2.1 reshape.89
  93.6 8.5 %multiply_convert_fusion.2 = bf16[2048,512]{1,0:T(8,128)(2,1)S(1)} fusion(bf16[2048,2048]{1,0:T(8,128)(2,1)} %all-gather.4.cloned.1.call-done, bf16[2048,512]{1,0:T(8,128)(2,1)} %param.14), kind=kOutput, calls=%fused_computation.47 | convolution fusion | flops 4297064448 | bytes 12582912 | tf_op jit(solution)/shard_map/dot_general | solution.py:95
  102.1 2.0 reshape.88
  104.1 137.0 %while.31 = (s32[]{:T(128)}, f32[4,128,128]{2,1,0:T(8,128)S(1)}, f32[4]{0:T(128)S(1)}, f32[4,512,4,128]{1,0,3,2:T(4,128)}, f32[4,512,4,128]{3,1,0,2:T(8,128)}, /...) while((s32[]{:T(128)}, f32[4,128,128]{2,1,0:T(8,128)S(1)}, ...), condition=%wide.region_3.4_spmd.clone.clone, body=%wide.region_0.3_spmd.clone.clone.sunk | while | flops 1350045696 | bytes 18760368 | solution.py:73
  104.1 1.2 reduce-window.16
  106.1 1.2 constant_dynamic-slice_fusion.5
  107.4 1.8 constant_dynamic-slice_fusion.6
  109.1 2.0 fusion.48
  111.1 1.4 fusion.49
  112.5 2.4 convolution_add_fusion.2
  114.9 1.1 copy.143
  116.0 21.0 %dynamic_update_slice.15 = f32[4,512,4,128]{1,0,3,2:T(4,128)} dynamic-update-slice(f32[4,512,4,128]{1,0,3,2:T(4,128)} %get-tuple-element.371, f32[1,512,4,128]{1,0,3,2:T(1,128)S(1)} %copy.143, s32[]{:T(128)S(6)} %copy.151, s32[]{:T(128)} %constant.52.clone.1..sunk.1, s32[]{:T(128)} %constant.52.clone.1..sunk.1, s32[]{:T(128)} %constant.52.clone.1..sunk.1) | dynamic-update-slice | bytes 2097156 | tf_op jit(solution)/shard_map/while/body/jit(dynamic_update_index_in_dim)/dynamic_update_slice | solution.py:73
  137.0 1.3 bitcast_dynamic-update-slice_fusion.2
  138.4 1.2 reduce-window.16
  140.4 1.2 constant_dynamic-slice_fusion.5
  141.6 1.8 constant_dynamic-slice_fusion.6
  143.4 2.0 fusion.48
  145.4 1.4 fusion.49
  146.7 2.4 convolution_add_fusion.2
  149.1 1.1 copy.143
  150.2 21.0 %dynamic_update_slice.15 = f32[4,512,4,128]{1,0,3,2:T(4,128)} dynamic-update-slice(f32[4,512,4,128]{1,0,3,2:T(4,128)} %get-tuple-element.371, f32[1,512,4,128]{1,0,3,2:T(1,128)S(1)} %copy.143, s32[]{:T(128)S(6)} %copy.151, s32[]{:T(128)} %constant.52.clone.1..sunk.1, s32[]{:T(128)} %constant.52.clone.1..sunk.1, s32[]{:T(128)} %constant.52.clone.1..sunk.1) | dynamic-update-slice | bytes 2097156 | tf_op jit(solution)/shard_map/while/body/jit(dynamic_update_index_in_dim)/dynamic_update_slice | solution.py:73
  171.3 1.3 bitcast_dynamic-update-slice_fusion.2
  172.6 1.2 reduce-window.16
  174.6 1.2 constant_dynamic-slice_fusion.5
  175.9 1.8 constant_dynamic-slice_fusion.6
  177.6 2.0 fusion.48
  179.6 1.4 fusion.49
  181.0 2.4 convolution_add_fusion.2
  183.4 1.1 copy.143
  184.5 21.0 %dynamic_update_slice.15 = f32[4,512,4,128]{1,0,3,2:T(4,128)} dynamic-update-slice(f32[4,512,4,128]{1,0,3,2:T(4,128)} %get-tuple-element.371, f32[1,512,4,128]{1,0,3,2:T(1,128)S(1)} %copy.143, s32[]{:T(128)S(6)} %copy.151, s32[]{:T(128)} %constant.52.clone.1..sunk.1, s32[]{:T(128)} %constant.52.clone.1..sunk.1, s32[]{:T(128)} %constant.52.clone.1..sunk.1) | dynamic-update-slice | bytes 2097156 | tf_op jit(solution)/shard_map/while/body/jit(dynamic_update_index_in_dim)/dynamic_update_slice | solution.py:73
  205.5 1.3 bitcast_dynamic-update-slice_fusion.2
  206.9 1.2 reduce-window.16
  208.9 1.2 constant_dynamic-slice_fusion.5
  210.1 1.8 constant_dynamic-slice_fusion.6
  211.9 2.0 fusion.48
  213.9 1.4 fusion.49
  215.2 2.4 convolution_add_fusion.2
  217.6 1.1 copy.143
  218.7 21.0 %dynamic_update_slice.15 = f32[4,512,4,128]{1,0,3,2:T(4,128)} dynamic-update-slice(f32[4,512,4,128]{1,0,3,2:T(4,128)} %get-tuple-element.371, f32[1,512,4,128]{1,0,3,2:T(1,128)S(1)} %copy.143, s32[]{:T(128)S(6)} %copy.151, s32[]{:T(128)} %constant.52.clone.1..sunk.1, s32[]{:T(128)} %constant.52.clone.1..sunk.1, s32[]{:T(128)} %constant.52.clone.1..sunk.1) | dynamic-update-slice | bytes 2097156 | tf_op jit(solution)/shard_map/while/body/jit(dynamic_update_index_in_dim)/dynamic_update_slice | solution.py:73
  239.8 1.3 bitcast_dynamic-update-slice_fusion.2
  241.4 9.8 %convolution_convert_fusion.2 = bf16[2048,512]{1,0:T(8,128)(2,1)} fusion(bf16[2048,2048]{1,0:T(8,128)(2,1)} %all-gather.4.cloned.1.call-done, bf16[2048,512]{1,0:T(8,128)(2,1)} %param.16), kind=kOutput, calls=%fused_computation.50 | convolution fusion | flops 4296015872 | bytes 12582912 | tf_op jit(solution)/shard_map/dot_general | solution.py:95
  251.2 4.4 %all-to-all-start = ((bf16[4,512,512]{2,1,0:T(8,128)(2,1)}), bf16[4,512,512]{2,1,0:T(8,128)(2,1)}, u32[]{:S(2)}, u32[]{:S(2)}) async-start(bf16[4,512,512]{2,1,0:T(8,128)(2,1)} %bitcast.2), calls=%async_computation | async-start | bytes 4194304 | tf_op jit(solution)/shard_map/all_to_all | solution.py:119
  255.7 4.9 %all-reduce = bf16[8]{0:T(256)(128)(2,1)S(1)} all-reduce(bf16[8]{0:T(256)(128)(2,1)S(1)} %dynamic-update-slice), channel_id=2, replica_groups=mesh['seq'=2,'mp'=4,'dp'=4] {'seq'}, use_global_device_ids=true, to_apply=%add | all-reduce | flops 8 | bytes 32
  260.7 5.7 %all-gather.1 = bf16[8,128,128]{2,1,0:T(8,128)(2,1)S(1)} all-gather(bf16[4,128,128]{2,1,0:T(8,128)(2,1)S(1)} %convert_element_type.89), channel_id=3, replica_groups=mesh['seq'=2,'mp'=4,'dp'=4] {'seq'}, dimensions={0}, use_global_device_ids=true | all-gather | bytes 393216 | tf_op jit(solution)/shard_map/all_gather | solution.py:12
  266.4 6.1 %reshape.91 = f32[2048,4,128]{0,2,1:T(8,128)} reshape(f32[4,512,4,128]{1,0,3,2:T(4,128)} %get-tuple-element.107) | data formatting | bytes 8388608 | tf_op jit(solution)/shard_map/reshape | solution.py:76
  272.5 8.8 %fusion.24 = bf16[2048,4,128]{0,2,1:T(8,128)(2,1)} fusion(f32[2048,4,128]{0,2,1:T(8,128)} %reshape.91, f32[4,128,128]{2,1,0:T(8,128)S(1)} %get-tuple-element.110, f32[2048,4,128]{2,0,1:T(8,128)} %bitcast.128), kind=kOutput, calls=%fused_computation.43 | convolution fusion | flops 1612709888 | bytes 10747904 | tf_op jit(solution)/shard_map/tha,hab->thb/dot_general | solution.py:113
  281.4 3.3 all_to_all.22
  284.7 1.7 copy.79
  286.4 3.6 %all-to-all-start.1 = ((bf16[4,512,512]{1,2,0:T(8,128)(2,1)}), bf16[4,512,512]{1,2,0:T(8,128)(2,1)S(1)}, u32[]{:S(2)}, u32[]{:S(2)}) async-start(bf16[4,512,512]{1,2,0:T(8,128)(2,1)} %copy.79), calls=%async_computation.1 | async-start | bytes 4194304 | tf_op jit(solution)/shard_map/all_to_all | solution.py:118
  290.0 2.2 convert_bitcast_fusion
  292.2 2.6 copy.94
  294.8 20.9 %all-to-all-done.1 = bf16[4,512,512]{1,2,0:T(8,128)(2,1)S(1)} async-done(((bf16[4,512,512]{1,2,0:T(8,128)(2,1)}), bf16[4,512,512]{1,2,0:T(8,128)(2,1)S(1)}, u32[]{:S(2)}, u32[]{:S(2)}) %all-to-all-start.1) | async-done | bytes 2097184 | tf_op jit(solution)/shard_map/all_to_all | solution.py:118
  315.7 0.5 multiply_reduce_fusion
  316.2 2.6 convert_element_type.105
  318.8 5.4 %copy.80 = f32[512,2048]{1,0:T(8,128)} copy(f32[512,2048]{0,1:T(8,128)} %bitcast.127) | data formatting | bytes 8388608 | tf_op jit(solution)/shard_map/convert_element_type | solution.py:121
  324.2 6.4 %multiply_convert_fusion.1 = bf16[512,2048]{1,0:T(8,128)(2,1)} fusion(f32[512,2048]{1,0:T(8,128)} %copy.80, f32[512,2048]{1,0:T(8,128)} %bitcast.126, f32[2048]{0:T(1024)S(1)} %copy-done.3, f32[512]{0:T(512)S(1)} %add_rsqrt_fusion), kind=kLoop, calls=%fused_computation.45 | loop fusion | flops 8388608 | bytes 10496000 | tf_op jit(solution)/shard_map/convert_element_type | solution.py:129
  (68 shorter events, 3.6 us)
Async XLA Ops:
  6.5 63.4 %copy-start = (bf16[2048,512]{1,0:T(8,128)(2,1)S(1)}, bf16[2048,512]{1,0:T(8,128)(2,1)}, u32[]{:S(2)}) copy-start(bf16[2048,512]{1,0:T(8,128)(2,1)} %param.13) | copy-start | bytes 6291460
  6.5 63.4 %all-gather.4.cloned.1.call-start = ((), (), s32[]{:S(2)}) async-start(), calls=%async_computation.2 | async-start | bytes 10485760 | tf_op jit(solution)/shard_map/all_gather | solution.py:92
  107.4 1.8 copy-start.2
  141.6 1.8 copy-start.2
  175.9 1.8 copy-start.2
  210.1 1.8 copy-start.2
  251.2 35.2 %all-to-all-start = ((bf16[4,512,512]{2,1,0:T(8,128)(2,1)}), bf16[4,512,512]{2,1,0:T(8,128)(2,1)}, u32[]{:S(2)}, u32[]{:S(2)}) async-start(bf16[4,512,512]{2,1,0:T(8,128)(2,1)} %bitcast.2), calls=%async_computation | async-start | bytes 4194304 | tf_op jit(solution)/shard_map/all_to_all | solution.py:119
  286.4 29.3 %all-to-all-start.1 = ((bf16[4,512,512]{1,2,0:T(8,128)(2,1)}), bf16[4,512,512]{1,2,0:T(8,128)(2,1)S(1)}, u32[]{:S(2)}, u32[]{:S(2)}) async-start(bf16[4,512,512]{1,2,0:T(8,128)(2,1)} %copy.79), calls=%async_computation.1 | async-start | bytes 4194304 | tf_op jit(solution)/shard_map/all_to_all | solution.py:118
  318.8 5.4 %copy-start.3 = (f32[2048]{0:T(1024)S(1)}, f32[2048]{0:T(1024)}, u32[]{:S(2)}) copy-start(f32[2048]{0:T(1024)} %param.19) | copy-start | bytes 24580
  324.2 6.4 %copy-start.1 = (bf16[2048,512]{1,0:T(8,128)(2,1)S(1)}, bf16[2048,512]{1,0:T(8,128)(2,1)}, u32[]{:S(2)}) copy-start(bf16[2048,512]{1,0:T(8,128)(2,1)} %param.13) | copy-start | bytes 6291460
Sparse Core Ops, SparseCore 0:
  8.9 60.9 all-gather.3
where the time goes:
time: 341 us; the launch traced here: 337 us
  local copies, waits for them, and re-layouts  131 us (38%)
  waiting for transfers between devices  80.8 us (24%)
  matrix products  67.6 us (20%)
  other arithmetic  25.1 us (7%)
  between operations  14.2 us (4%)
  blocking collectives  10.7 us (3%)
  starting transfers between devices  8.06 us (2%)
    dynamic_update_slice x8, local copies, waits for them, and re-layouts, run_blocks(): lax.scan(advance, initial, (shaped(queries), shaped(key_rows), shaped(val...  88.5 us
    all_gather x1, waiting for transfers between devices, body(): piece = lax.all_gather(tokens, 'mp', axis=1, tiled=True)  59.2 us
    dot_general x4, matrix products, body(): results.append(jnp.dot(piece, weight, preferred_element_type=jnp.float32))  35.9 us
    all_to_all x1, waiting for transfers between devices, body(): lax.all_to_all(output, 'mp', split_axis=0, concat_axis=1, tiled=True)  20.9 us
    dynamic_slice x8, local copies, waits for them, and re-layouts, run_blocks(): lax.scan(advance, initial, (shaped(queries), shaped(key_rows), shaped(val...  11.9 us
    dot_general x4, matrix products, advance(): jnp.einsum('sha,shb->hab', key_scaled, value_blk.astype(jnp.float32), pre...  9.56 us
    dot_general x1, matrix products, body(): jnp.einsum('tha,hab->thb', query_device, incoming, precision=lax.Precisio...  8.83 us
    reshape x3, local copies, waits for them, and re-layouts, shaped(): return source.reshape(block_count, block_rows, head_count, head_width)  8.09 us
  transfers between devices with their start and end apart: 3, of which 2 were waited for; matrix products, arithmetic and copies ran while one was open for 7% of the time, Pallas kernels for 0%

commit v1 on v0

--- a/solution.py
+++ b/solution.py
@@ -115,7 +115,10 @@
     )
     output = (local_part + from_before).astype(jnp.bfloat16).reshape(seq_rows, local_width)
     moved_output, moved_gate = (
-        lax.all_to_all(output, "mp", split_axis=0, concat_axis=1, tiled=True),
+        jnp.concatenate(
+            lax.all_to_all(jnp.stack(jnp.split(output, lax.axis_size("mp"), axis=0)), "mp", 0, 0),
+            axis=1,
+        ),
         lax.all_to_all(gate, "mp", split_axis=0, concat_axis=1, tiled=True),
     )
     output_float = moved_output.astype(jnp.float32)

time: 341 us -> 336 us (0.985)
  local copies, waits for them, and re-layouts: 131 us -> 126 us
    all_to_all x2 -> x0, local copies, waits for them, and re-layouts: 5.04 us -> none  [body(): lax.all_to_all(output, 'mp', split_axis=0, concat_axis=1, tiled=True)]
    another operation x10 -> x11, other arithmetic: 5.59 us -> 7.17 us
where the time goes in v1:
time: 336 us; the launch traced here: 333 us
  local copies, waits for them, and re-layouts  126 us (38%)
  waiting for transfers between devices  80.8 us (24%)
  matrix products  66.3 us (20%)
  other arithmetic  26.7 us (8%)
  between operations  14.2 us (4%)
  blocking collectives  10.7 us (3%)
  starting transfers between devices  8.06 us (2%)
    dynamic_update_slice x8, local copies, waits for them, and re-layouts, run_blocks(): lax.scan(advance, initial, (shaped(queries), shaped(key_rows), shaped(val...  88.5 us
    all_gather x1, waiting for transfers between devices, body(): piece = lax.all_gather(tokens, 'mp', axis=1, tiled=True)  59.2 us
    dot_general x4, matrix products, body(): results.append(jnp.dot(piece, weight, preferred_element_type=jnp.float32))  35.9 us
    all_to_all x1, waiting for transfers between devices, body(): lax.all_to_all(jnp.stack(jnp.split(output, lax.axis_size('mp'), axis=0)),...  20.9 us
    dynamic_slice x8, local copies, waits for them, and re-layouts, run_blocks(): lax.scan(advance, initial, (shaped(queries), shaped(key_rows), shaped(val...  11.9 us
    dot_general x4, matrix products, advance(): jnp.einsum('sha,shb->hab', key_scaled, value_blk.astype(jnp.float32), pre...  9.56 us
    reshape x3, local copies, waits for them, and re-layouts, shaped(): return source.reshape(block_count, block_rows, head_count, head_width)  8.09 us
    dot_general x4, matrix products, advance(): jnp.einsum('hts,shb->thb', scores, value_blk, preferred_element_type=jnp....  7.92 us
  transfers between devices with their start and end apart: 3, of which 2 were waited for; matrix products, arithmetic and copies ran while one was open for 7% of the time, Pallas kernels for 0%

profile of v1, /device:TPU:0, one launch (start us, length us, event | category | flops | bytes accessed | tf_op | source)
XLA Modules:
  0.0 333.1 jit_solution(903982858529448653)
XLA Ops:
  6.5 0.7 all-gather.4.cloned.1.call-update
  7.3 1.2 dynamic-slice
  9.2 0.7 negate_log-plus-one_fusion
  9.9 0.8 broadcast_subtract_fusion
  10.7 59.2 %all-gather.4.cloned.1.call-done = bf16[2048,2048]{1,0:T(8,128)(2,1)} async-done(((bf16[2048,512]{1,0:T(8,128)(2,1)}), bf16[2048,2048]{1,0:T(8,128)(2,1)}) %all-gather.4.cloned.1.call-update) | async-done | bytes 8388624 | tf_op jit(solution)/shard_map/all_gather | solution.py:92
  69.9 9.1 %convolution_convert_fusion = bf16[2048,512]{1,0:T(8,128)(2,1)} fusion(bf16[2048,2048]{1,0:T(8,128)(2,1)} %all-gather.4.cloned.1.call-done, bf16[2048,512]{1,0:T(8,128)(2,1)S(1)} %copy-done), kind=kOutput, calls=%fused_computation.48 | convolution fusion | flops 4296015872 | bytes 12582912 | tf_op jit(solution)/shard_map/dot_general | solution.py:95
  79.0 4.0 %reshape.96 = bf16[4,512,4,128]{3,2,1,0:T(4,128)(2,1)} reshape(bf16[2048,512]{1,0:T(8,128)(2,1)} %convolution_convert_fusion) | data formatting | bytes 4194304 | tf_op jit(solution)/shard_map/reshape | solution.py:35
  83.0 8.5 %convolution_convert_fusion.1 = bf16[2048,512]{1,0:T(8,128)(2,1)S(1)} fusion(bf16[2048,2048]{1,0:T(8,128)(2,1)} %all-gather.4.cloned.1.call-done, bf16[2048,512]{1,0:T(8,128)(2,1)} %param.15), kind=kOutput, calls=%fused_computation.49 | convolution fusion | flops 4296015872 | bytes 12582912 | tf_op jit(solution)/shard_map/dot_general | solution.py:95
  91.5 2.1 reshape.95
  93.6 8.5 %multiply_convert_fusion.2 = bf16[2048,512]{1,0:T(8,128)(2,1)S(1)} fusion(bf16[2048,2048]{1,0:T(8,128)(2,1)} %all-gather.4.cloned.1.call-done, bf16[2048,512]{1,0:T(8,128)(2,1)} %param.14), kind=kOutput, calls=%fused_computation.47 | convolution fusion | flops 4297064448 | bytes 12582912 | tf_op jit(solution)/shard_map/dot_general | solution.py:95
  102.1 2.0 reshape.94
  104.1 137.0 %while.31 = (s32[]{:T(128)}, f32[4,128,128]{2,1,0:T(8,128)S(1)}, f32[4]{0:T(128)S(1)}, f32[4,512,4,128]{1,0,3,2:T(4,128)}, f32[4,512,4,128]{3,1,0,2:T(8,128)}, /...) while((s32[]{:T(128)}, f32[4,128,128]{2,1,0:T(8,128)S(1)}, ...), condition=%wide.region_3.4_spmd.clone.clone, body=%wide.region_0.3_spmd.clone.clone.sunk | while | flops 1350045696 | bytes 18760368 | solution.py:73
  104.1 1.2 reduce-window.16
  106.1 1.2 constant_dynamic-slice_fusion.5
  107.4 1.8 constant_dynamic-slice_fusion.6
  109.1 2.0 fusion.49
  111.1 1.4 fusion.50
  112.5 2.4 convolution_add_fusion.2
  114.9 1.1 copy.141
  116.0 21.0 %dynamic_update_slice.15 = f32[4,512,4,128]{1,0,3,2:T(4,128)} dynamic-update-slice(f32[4,512,4,128]{1,0,3,2:T(4,128)} %get-tuple-element.375, f32[1,512,4,128]{1,0,3,2:T(1,128)S(1)} %copy.141, s32[]{:T(128)S(6)} %copy.149, s32[]{:T(128)} %constant.52.clone.1..sunk.1, s32[]{:T(128)} %constant.52.clone.1..sunk.1, s32[]{:T(128)} %constant.52.clone.1..sunk.1) | dynamic-update-slice | bytes 2097156 | tf_op jit(solution)/shard_map/while/body/jit(dynamic_update_index_in_dim)/dynamic_update_slice | solution.py:73
  137.0 1.3 bitcast_dynamic-update-slice_fusion.2
  138.4 1.2 reduce-window.16
  140.4 1.2 constant_dynamic-slice_fusion.5
  141.6 1.8 constant_dynamic-slice_fusion.6
  143.4 2.0 fusion.49
  145.4 1.4 fusion.50
  146.7 2.4 convolution_add_fusion.2
  149.1 1.1 copy.141
  150.2 21.0 %dynamic_update_slice.15 = f32[4,512,4,128]{1,0,3,2:T(4,128)} dynamic-update-slice(f32[4,512,4,128]{1,0,3,2:T(4,128)} %get-tuple-element.375, f32[1,512,4,128]{1,0,3,2:T(1,128)S(1)} %copy.141, s32[]{:T(128)S(6)} %copy.149, s32[]{:T(128)} %constant.52.clone.1..sunk.1, s32[]{:T(128)} %constant.52.clone.1..sunk.1, s32[]{:T(128)} %constant.52.clone.1..sunk.1) | dynamic-update-slice | bytes 2097156 | tf_op jit(solution)/shard_map/while/body/jit(dynamic_update_index_in_dim)/dynamic_update_slice | solution.py:73
  171.3 1.3 bitcast_dynamic-update-slice_fusion.2
  172.6 1.2 reduce-window.16
  174.6 1.2 constant_dynamic-slice_fusion.5
  175.9 1.8 constant_dynamic-slice_fusion.6
  177.6 2.0 fusion.49
  179.6 1.4 fusion.50
  181.0 2.4 convolution_add_fusion.2
  183.4 1.1 copy.141
  184.5 21.0 %dynamic_update_slice.15 = f32[4,512,4,128]{1,0,3,2:T(4,128)} dynamic-update-slice(f32[4,512,4,128]{1,0,3,2:T(4,128)} %get-tuple-element.375, f32[1,512,4,128]{1,0,3,2:T(1,128)S(1)} %copy.141, s32[]{:T(128)S(6)} %copy.149, s32[]{:T(128)} %constant.52.clone.1..sunk.1, s32[]{:T(128)} %constant.52.clone.1..sunk.1, s32[]{:T(128)} %constant.52.clone.1..sunk.1) | dynamic-update-slice | bytes 2097156 | tf_op jit(solution)/shard_map/while/body/jit(dynamic_update_index_in_dim)/dynamic_update_slice | solution.py:73
  205.5 1.3 bitcast_dynamic-update-slice_fusion.2
  206.9 1.2 reduce-window.16
  208.9 1.2 constant_dynamic-slice_fusion.5
  210.1 1.8 constant_dynamic-slice_fusion.6
  211.9 2.0 fusion.49
  213.9 1.4 fusion.50
  215.2 2.4 convolution_add_fusion.2
  217.6 1.1 copy.141
  218.7 21.0 %dynamic_update_slice.15 = f32[4,512,4,128]{1,0,3,2:T(4,128)} dynamic-update-slice(f32[4,512,4,128]{1,0,3,2:T(4,128)} %get-tuple-element.375, f32[1,512,4,128]{1,0,3,2:T(1,128)S(1)} %copy.141, s32[]{:T(128)S(6)} %copy.149, s32[]{:T(128)} %constant.52.clone.1..sunk.1, s32[]{:T(128)} %constant.52.clone.1..sunk.1, s32[]{:T(128)} %constant.52.clone.1..sunk.1) | dynamic-update-slice | bytes 2097156 | tf_op jit(solution)/shard_map/while/body/jit(dynamic_update_index_in_dim)/dynamic_update_slice | solution.py:73
  239.8 1.3 bitcast_dynamic-update-slice_fusion.2
  241.1 0.2 dynamic-update-slice
  241.4 9.8 %convolution_convert_fusion.2 = bf16[2048,512]{1,0:T(8,128)(2,1)} fusion(bf16[2048,2048]{1,0:T(8,128)(2,1)} %all-gather.4.cloned.1.call-done, bf16[2048,512]{1,0:T(8,128)(2,1)} %param.16), kind=kOutput, calls=%fused_computation.50 | convolution fusion | flops 4296015872 | bytes 12582912 | tf_op jit(solution)/shard_map/dot_general | solution.py:95
  251.2 4.4 %all-to-all-start = ((bf16[4,512,512]{2,1,0:T(8,128)(2,1)}), bf16[4,512,512]{2,1,0:T(8,128)(2,1)}, u32[]{:S(2)}, u32[]{:S(2)}) async-start(bf16[4,512,512]{2,1,0:T(8,128)(2,1)} %bitcast.2), calls=%async_computation | async-start | bytes 4194304 | tf_op jit(solution)/shard_map/all_to_all | solution.py:122
  255.7 4.9 %all-reduce = bf16[8]{0:T(256)(128)(2,1)S(1)} all-reduce(bf16[8]{0:T(256)(128)(2,1)S(1)} %dynamic-update-slice), channel_id=2, replica_groups=mesh['seq'=2,'mp'=4,'dp'=4] {'seq'}, use_global_device_ids=true, to_apply=%add | all-reduce | flops 8 | bytes 32
  260.7 5.7 %all-gather.1 = bf16[8,128,128]{2,1,0:T(8,128)(2,1)S(1)} all-gather(bf16[4,128,128]{2,1,0:T(8,128)(2,1)S(1)} %convert_element_type.89), channel_id=3, replica_groups=mesh['seq'=2,'mp'=4,'dp'=4] {'seq'}, dimensions={0}, use_global_device_ids=true | all-gather | bytes 393216 | tf_op jit(solution)/shard_map/all_gather | solution.py:12
  266.5 6.3 %reshape.97 = f32[2048,4,128]{0,2,1:T(8,128)} reshape(f32[4,512,4,128]{1,0,3,2:T(4,128)} %get-tuple-element.107) | data formatting | bytes 8388608 | tf_op jit(solution)/shard_map/reshape | solution.py:76
  272.8 7.5 %fusion.24 = bf16[2048,4,128]{0,2,1:T(8,128)(2,1)S(1)} fusion(f32[2048,4,128]{0,2,1:T(8,128)} %reshape.97, f32[4,128,128]{2,1,0:T(8,128)S(1)} %get-tuple-element.110, f32[2048,4,128]{2,0,1:T(8,128)} %bitcast.130), kind=kOutput, calls=%fused_computation.43 | convolution fusion | flops 1612709888 | bytes 10747904 | tf_op jit(solution)/shard_map/tha,hab->thb/dot_general | solution.py:113
  280.5 1.6 pad_maximum_fusion
  282.1 3.6 %all-to-all-start.1 = ((bf16[4,512,512]{1,2,0:T(8,128)(2,1)}), bf16[4,512,512]{1,2,0:T(8,128)(2,1)S(1)}, u32[]{:S(2)}, u32[]{:S(2)}) async-start(bf16[4,512,512]{1,2,0:T(8,128)(2,1)} %pad_maximum_fusion), calls=%async_computation.1 | async-start | bytes 4194304 | tf_op jit(solution)/shard_map/all_to_all | solution.py:119
  285.7 2.2 convert_bitcast_fusion
  287.9 2.6 copy.92
  290.4 20.9 %all-to-all-done.1 = bf16[4,512,512]{1,2,0:T(8,128)(2,1)S(1)} async-done(((bf16[4,512,512]{1,2,0:T(8,128)(2,1)}), bf16[4,512,512]{1,2,0:T(8,128)(2,1)S(1)}, u32[]{:S(2)}, u32[]{:S(2)}) %all-to-all-start.1) | async-done | bytes 2097184 | tf_op jit(solution)/shard_map/all_to_all | solution.py:119
  311.3 0.5 multiply_reduce_fusion
  311.8 2.6 convert_element_type.105
  314.4 5.4 %copy.82 = f32[512,2048]{1,0:T(8,128)} copy(f32[512,2048]{0,1:T(8,128)} %bitcast.129) | data formatting | bytes 8388608 | tf_op jit(solution)/shard_map/convert_element_type | solution.py:124
  319.8 6.4 %multiply_convert_fusion.1 = bf16[512,2048]{1,0:T(8,128)(2,1)} fusion(f32[512,2048]{1,0:T(8,128)} %copy.82, f32[512,2048]{1,0:T(8,128)} %bitcast.128, f32[2048]{0:T(1024)S(1)} %copy-done.3, f32[512]{0:T(512)S(1)} %add_rsqrt_fusion), kind=kLoop, calls=%fused_computation.45 | loop fusion | flops 8388608 | bytes 10496000 | tf_op jit(solution)/shard_map/convert_element_type | solution.py:132
  (68 shorter events, 3.6 us)
Async XLA Ops:
  6.5 63.4 %copy-start = (bf16[2048,512]{1,0:T(8,128)(2,1)S(1)}, bf16[2048,512]{1,0:T(8,128)(2,1)}, u32[]{:S(2)}) copy-start(bf16[2048,512]{1,0:T(8,128)(2,1)} %param.13) | copy-start | bytes 6291460
  6.5 63.4 %all-gather.4.cloned.1.call-start = ((), (), s32[]{:S(2)}) async-start(), calls=%async_computation.2 | async-start | bytes 10485760 | tf_op jit(solution)/shard_map/all_gather | solution.py:92
  107.4 1.8 copy-start.2
  141.6 1.8 copy-start.2
  175.9 1.8 copy-start.2
  210.1 1.8 copy-start.2
  251.2 30.9 %all-to-all-start = ((bf16[4,512,512]{2,1,0:T(8,128)(2,1)}), bf16[4,512,512]{2,1,0:T(8,128)(2,1)}, u32[]{:S(2)}, u32[]{:S(2)}) async-start(bf16[4,512,512]{2,1,0:T(8,128)(2,1)} %bitcast.2), calls=%async_computation | async-start | bytes 4194304 | tf_op jit(solution)/shard_map/all_to_all | solution.py:122
  282.1 29.3 %all-to-all-start.1 = ((bf16[4,512,512]{1,2,0:T(8,128)(2,1)}), bf16[4,512,512]{1,2,0:T(8,128)(2,1)S(1)}, u32[]{:S(2)}, u32[]{:S(2)}) async-start(bf16[4,512,512]{1,2,0:T(8,128)(2,1)} %pad_maximum_fusion), calls=%async_computation.1 | async-start | bytes 4194304 | tf_op jit(solution)/shard_map/all_to_all | solution.py:119
  314.4 5.4 %copy-start.3 = (f32[2048]{0:T(1024)S(1)}, f32[2048]{0:T(1024)}, u32[]{:S(2)}) copy-start(f32[2048]{0:T(1024)} %param.19) | copy-start | bytes 24580
  319.8 6.4 %copy-start.1 = (bf16[2048,512]{1,0:T(8,128)(2,1)S(1)}, bf16[2048,512]{1,0:T(8,128)(2,1)}, u32[]{:S(2)}) copy-start(bf16[2048,512]{1,0:T(8,128)(2,1)} %param.13) | copy-start | bytes 6291460
Sparse Core Ops, SparseCore 0:
  8.9 60.9 all-gather.3
